TPU v7x, 32 devices: a whole 2x2x4 slice. The times are simulated.
32 devices in a mesh: dp: 32 (over z, y, x, core).
Axes of the slice: x: 2, y: 2, z: 4, core: 2. Of those that a mesh axis runs over, the one named last changes fastest.
Arguments:
- features: bfloat16 [32768, 3136], P('dp'), may hold values from -6 to 6
- w_one: bfloat16 [512, 3136], replicated, may hold values from -0.109375 to 0.109375
- b_one: float32 [512], replicated, may hold values from -3 to 3
- w_two: bfloat16 [512, 918], replicated, may hold values from -0.25 to 0.25
- b_two: float32 [918], replicated, may hold values from -112 to 112
- action: int32 [32768], P('dp'), may hold values from 0 to 17
- target_probs: float32 [32768, 18, 51], P('dp'), may hold values from 0 to 1, as said below
- next_action: int32 [32768], P('dp'), may hold values from 0 to 17
- lower_idx: int32 [32768, 51], P('dp'), may hold values from 0 to 49
- upper_frac: float32 [32768, 51], P('dp'), may hold values from 0 to 1
- is_weight: float32 [32768], P('dp'), may hold values from 0.1 to 1
Outputs:
- grad_w1: float32 [512, 3136], replicated
- grad_b1: float32 [512], replicated
- grad_w2: float32 [512, 918], replicated
- grad_b2: float32 [918], replicated
- mean_loss: float32 [], replicated
- priorities: float32 [32768], P('dp')
Inputs may be any that keep to these rules, and one draw needn't show every extreme that they name: Each target_probs[i, a] is a distribution over the atoms: positive entries that sum to one.
All inputs are finite; a program needn't handle non-finite values.
Results may differ from a plain program's by a relative error of at most 0.005.
Values sent between devices are 32-bit elements; how exact they have to be, the bound alone decides.
A program may use at most 128 MiB of HBM per device.

v0:
```python
import jax
import jax.numpy as jnp
from jax import lax
from jax.sharding import PartitionSpec as P


def forward_loss(
    features,
    w_one,
    b_one,
    w_two,
    b_two,
    action,
    target_probs,
    next_action,
    lower_idx,
    upper_frac,
    is_weight,
):
    row_count = features.shape[0]
    n_act = target_probs.shape[1]
    n_atom = target_probs.shape[2]
    pre_act = (
        lax.dot_general(
            features, w_one, (((1,), (1,)), ((), ())), preferred_element_type=jnp.float32
        )
        + b_one
    )
    hidden = jnp.maximum(pre_act, 0.0).astype(jnp.bfloat16)
    logits = (jnp.dot(hidden, w_two, preferred_element_type=jnp.float32) + b_two).reshape(
        row_count, n_act, n_atom
    )
    chosen = jnp.take_along_axis(logits, action[:, None, None], axis=1)[:, 0, :]
    log_probs = jax.nn.log_softmax(chosen, axis=-1)
    next_probs = jnp.take_along_axis(target_probs, next_action[:, None, None], axis=1)[:, 0, :]
    atom_ids = jnp.arange(n_atom, dtype=jnp.int32)
    mass_low = next_probs * (1.0 - upper_frac)
    mass_high = next_probs * upper_frac
    low_hot = lower_idx[:, :, None] == atom_ids[None, None, :]
    high_hot = lower_idx[:, :, None] + 1 == atom_ids[None, None, :]
    projected = jnp.sum(
        jnp.where(low_hot, mass_low[:, :, None], 0.0)
        + jnp.where(high_hot, mass_high[:, :, None], 0.0),
        axis=1,
    )
    cross_ent = -jnp.sum(projected * log_probs, axis=-1)
    grad_chosen = is_weight[:, None] * (
        jnp.exp(log_probs) * jnp.sum(projected, axis=-1, keepdims=True) - projected
    )
    act_hot = action[:, None] == jnp.arange(n_act, dtype=jnp.int32)[None, :]
    grad_logits = (
        jnp.where(act_hot[:, :, None], grad_chosen[:, None, :], 0.0)
        .reshape(row_count, n_act * n_atom)
        .astype(jnp.bfloat16)
    )
    grad_hidden = lax.dot_general(
        grad_logits, w_two, (((1,), (1,)), ((), ())), preferred_element_type=jnp.float32
    )
    grad_pre = jnp.where(pre_act > 0.0, grad_hidden, 0.0).astype(jnp.bfloat16)
    return (hidden, grad_logits, grad_pre, cross_ent)


def on_device(
    features,
    w_one,
    b_one,
    w_two,
    b_two,
    action,
    target_probs,
    next_action,
    lower_idx,
    upper_frac,
    is_weight,
):
    total_rows = features.shape[0] * lax.axis_size("dp")
    hidden, grad_logits, grad_pre, cross_ent = forward_loss(
        features,
        w_one,
        b_one,
        w_two,
        b_two,
        action,
        target_probs,
        next_action,
        lower_idx,
        upper_frac,
        is_weight,
    )
    local_loss = jnp.sum(is_weight * cross_ent)
    local_top = jnp.max(cross_ent)
    loss_sum = lax.psum(local_loss, "dp")
    top = lax.pmax(local_top, "dp")
    local_w2 = lax.dot_general(
        hidden, grad_logits, (((0,), (0,)), ((), ())), preferred_element_type=jnp.float32
    )
    local_b2 = jnp.sum(grad_logits.astype(jnp.float32), axis=0)
    local_b1 = jnp.sum(grad_pre.astype(jnp.float32), axis=0)
    grad_b1, grad_w2, grad_b2 = lax.psum((local_b1, local_w2, local_b2), "dp")
    local_w1 = lax.dot_general(
        grad_pre, features, (((0,), (0,)), ((), ())), preferred_element_type=jnp.float32
    )
    grad_w1 = lax.psum(local_w1, "dp")
    priorities = cross_ent / jnp.maximum(top, 1.0)
    mean_loss = loss_sum / total_rows
    return (grad_w1, grad_b1, grad_w2, grad_b2, mean_loss, priorities)


def solution(mesh):
    in_specs = (
        P("dp", None),
        P(),
        P(),
        P(),
        P(),
        P("dp"),
        P("dp", None, None),
        P("dp"),
        P("dp", None),
        P("dp", None),
        P("dp"),
    )
    out_specs = (P(), P(), P(), P(), P(), P("dp"))
    return jax.shard_map(
        on_device, mesh=mesh, in_specs=in_specs, out_specs=out_specs, check_vma=False
    )
```

profile of v0, /device:TPU:0, one launch (start us, length us, event | category | flops | bytes accessed | tf_op | source)
XLA Modules:
  0.0 283.7 jit_solution(31237595956415352)
XLA Ops:
  7.2 0.9 and_reduce_fusion
  8.1 0.8 iota_compare_fusion.2
  8.9 0.7 and_reduce_fusion.1
  9.6 1.0 broadcast_add_fusion
  10.6 5.9 %fusion.16 = f32[1024,512]{1,0:T(8,128)S(1)} fusion(bf16[1024,3136]{0,1:T(8,128)(2,1)} %param.13, bf16[512,3136]{0,1:T(8,128)(2,1)S(1)} %copy-done), kind=kOutput, calls=%fused_computation.50 | convolution fusion | flops 3288334336 | bytes 11730944 | tf_op jit(solution)/shard_map/dot_general | solution.py:24
  16.5 1.3 copy-done.10
  17.8 3.0 %convolution_add_fusion = f32[1024,918]{0,1:T(8,128)} fusion(bf16[512,918]{0,1:T(8,128)(2,1)S(1)} %copy-done.7, f32[918]{0:T(1024)S(1)} %copy-done.8, f32[1024,512]{1,0:T(8,128)S(1)} %fusion.16, f32[512]{0:T(512)S(1)} %copy-done.9), kind=kOutput, calls=%fused_computation.12 | convolution fusion | flops 965105664 | bytes 6803032 | tf_op jit(solution)/shard_map/dot_general | solution.py:30
  20.8 3.9 %reshape.118 = f32[1024,18,51]{0,2,1:T(8,128)} reshape(f32[1024,918]{0,1:T(8,128)} %convolution_add_fusion) | data formatting | bytes 7520256 | tf_op jit(solution)/shard_map/reshape | solution.py:30
  24.7 7.5 %copy.39 = f32[1024,18,51]{2,0,1:T(8,128)} copy(f32[1024,18,51]{0,2,1:T(8,128)} %reshape.118) | data formatting | bytes 7520256 | tf_op jit(solution)/shard_map/reshape | solution.py:30
  32.2 10.6 %gather_fusion = f32[1024,51]{1,0:T(8,128)S(1)} fusion(f32[1024,18,51]{2,0,1:T(8,128)} %copy.39, s32[1024]{0:T(1024)S(1)} %bitcast.54), kind=kCustom, calls=%fused_computation.clone | custom fusion | bytes 425984 | tf_op jit(solution)/shard_map/jit(take_along_axis)/gather | solution.py:33
  43.7 7.5 %copy.40 = f32[1024,18,51]{2,0,1:T(8,128)} copy(f32[1024,18,51]{0,2,1:T(8,128)} %param.19) | data formatting | bytes 7520256 | tf_op args[6]
  51.2 10.5 %gather_fusion.1 = f32[1024,51]{1,0:T(8,128)S(1)} fusion(f32[1024,18,51]{2,0,1:T(8,128)} %copy.40, s32[1024]{0:T(1024)S(1)} %bitcast.53), kind=kCustom, calls=%fused_computation.1.clone | custom fusion | bytes 425984 | tf_op jit(solution)/shard_map/jit(take_along_axis)/gather | solution.py:35
  62.0 4.5 %fusion.1 = (f32[1024]{0:T(1024)S(1)}, f32[1024,51]{0,1:T(8,128)S(1)}) fusion(f32[1024,51]{0,1:T(8,128)S(1)} %get-tuple-element.21, s32[1024,51]{0,1:T(8,128)S(1)} %broadcast_add_fusion, f32[1024,51]{0,1:T(8,128)S(1)} %get-tuple-element.20, s32[1024,51]{0,1:T(8,128)S(1)} %copy-done.4), kind=kLoop, calls=%fused_computation.5 | loop fusion | flops 18590720 | bytes 1048576 | tf_op jit(solution)/shard_map/reduce_sum | solution.py:48
  66.7 1.1 fusion.3
  68.3 1.8 convert_element_type.22
  70.1 3.9 %convert_reduce_fusion.1 = (f32[512]{0:T(512)S(1)}, bf16[1024,512]{1,0:T(8,128)(2,1)S(1)}) fusion(bf16[1024,918]{0,1:T(8,128)(2,1)} %convert_element_type.22, bf16[512,918]{0,1:T(8,128)(2,1)} %param.16, f32[1024,512]{1,0:T(8,128)} %copy-done.10, f32[512]{0:T(512)S(1)} %copy-done.9), kind=kOutput, calls=%fused_computation.9 | convolution fusion | flops 965737984 | bytes 5969920 | tf_op jit(solution)/shard_map/dot_general | solution.py:56
  74.1 2.4 fusion.5
  76.5 8.2 %fusion.17 = f32[512,3136]{0,1:T(8,128)} fusion(bf16[1024,3136]{0,1:T(8,128)(2,1)} %param.13, bf16[1024,512]{1,0:T(8,128)(2,1)S(1)} %get-tuple-element.25), kind=kOutput, calls=%fused_computation.51 | convolution fusion | flops 3288334336 | bytes 13893632 | tf_op jit(solution)/shard_map/dot_general | solution.py:100
  84.7 0.6 multiply_reduce_fusion
  85.9 43.8 %pmax.7 = f32[]{:T(128)} all-reduce(f32[]{:T(128)} %get-tuple-element.9), channel_id=1, replica_groups=mesh['dp'=32] {'dp'}, use_global_device_ids=true, to_apply=%region_14.16 | all-reduce | flops 1 | bytes 8 | tf_op jit(solution)/shard_map/pmax | solution.py:93
  131.0 41.0 %all-reduce = (f32[512]{0:T(512)}, f32[918]{0:T(1024)}, f32[]{:T(128)}) all-reduce(f32[512]{0:T(512)S(1)} %get-tuple-element.24, f32[918]{0:T(1024)S(1)} %reduce_sum.74, f32[]{:T(128)} %get-tuple-element.10), channel_id=1, replica_groups=mesh['dp'=32] {'dp'}, use_global_device_ids=true, to_apply=%region_6.8 | all-reduce | flops 1431 | bytes 11448 | tf_op jit(solution)/shard_map/psum | solution.py:99
  173.2 94.7 %all-reduce.4.cloned.1.call-done = (f32[512,3136]{0,1:T(8,128)}, f32[512,918]{0,1:T(8,128)}) async-done(((f32[512,3136]{0,1:T(8,128)}, f32[512,918]{0,1:T(8,128)}), (f32[512,3136]{0,1:T(8,128)}, f32[512,918]{0,1:T(8,128)})) %all-reduce.4.cloned.1.call-update) | async-done | bytes 8302608 | tf_op jit(solution)/shard_map/psum | solution.py:103
  268.0 6.5 %copy.47 = f32[512,3136]{0,1:T(8,128)} copy(f32[512,3136]{0,1:T(8,128)} %get-tuple-element.28) | data formatting | bytes 12845056
  274.5 1.2 copy.48
  (40 shorter events, 3.8 us)
Async XLA Ops:
  7.2 3.4 %copy-start = (bf16[512,3136]{0,1:T(8,128)(2,1)S(1)}, bf16[512,3136]{0,1:T(8,128)(2,1)}, u32[]{:S(2)}) copy-start(bf16[512,3136]{0,1:T(8,128)(2,1)} %param.14) | copy-start | bytes 9633796
  7.2 260.8 %all-reduce.4.cloned.1.call-start = ((), (), s32[]{:S(2)}) async-start(), calls=%async_computation | async-start | bytes 16613376 | tf_op jit(solution)/shard_map/psum | solution.py:103
  10.5 7.3 %copy-start.7 = (bf16[512,918]{0,1:T(8,128)(2,1)S(1)}, bf16[512,918]{0,1:T(8,128)(2,1)}, u32[]{:S(2)}) copy-start(bf16[512,918]{0,1:T(8,128)(2,1)} %param.16) | copy-start | bytes 2820100
  10.6 7.3 %copy-start.8 = (f32[918]{0:T(1024)S(1)}, f32[918]{0:T(1024)}, u32[]{:S(2)}) copy-start(f32[918]{0:T(1024)} %param.17) | copy-start | bytes 11020
  10.6 7.2 %copy-start.9 = (f32[512]{0:T(512)S(1)}, f32[512]{0:T(512)}, u32[]{:S(2)}) copy-start(f32[512]{0:T(512)} %param.15) | copy-start | bytes 6148
  16.5 1.3 copy-start.10
  51.2 10.8 %copy-start.5 = (f32[1024,51]{0,1:T(8,128)S(1)}, f32[1024,51]{0,1:T(8,128)}, u32[]{:S(2)}) copy-start(f32[1024,51]{0,1:T(8,128)} %param.22) | copy-start | bytes 626692
  51.2 10.8 %copy-start.4 = (s32[1024,51]{0,1:T(8,128)S(1)}, s32[1024,51]{0,1:T(8,128)}, u32[]{:S(2)}) copy-start(s32[1024,51]{0,1:T(8,128)} %param.21) | copy-start | bytes 626692
  61.7 5.0 %copy-start.6 = (f32[1024]{0:T(1024)S(1)}, f32[1024]{0:T(1024)}, u32[]{:S(2)}) copy-start(f32[1024]{0:T(1024)} %param.23) | copy-start | bytes 12292
  70.1 3.9 %copy-start.3 = (bf16[1024,918]{0,1:T(8,128)(2,1)S(1)}, bf16[1024,918]{0,1:T(8,128)(2,1)}, u32[]{:S(2)}) copy-start(bf16[1024,918]{0,1:T(8,128)(2,1)} %convert_element_type.22) | copy-start | bytes 5640196
  70.1 3.9 %copy-start.11 = (f32[1024,512]{1,0:T(8,128)S(1)}, f32[1024,512]{1,0:T(8,128)}, u32[]{:S(2)}) copy-start(f32[1024,512]{1,0:T(8,128)} %copy-done.10) | copy-start | bytes 6291460
  268.0 6.5 %copy-start.2 = (f32[512,918]{0,1:T(8,128)S(1)}, f32[512,918]{0,1:T(8,128)}, u32[]{:S(2)}) copy-start(f32[512,918]{0,1:T(8,128)} %get-tuple-element.30) | copy-start | bytes 5640196
  268.0 7.7 %copy-start.1 = (bf16[512,3136]{0,1:T(8,128)(2,1)S(1)}, bf16[512,3136]{0,1:T(8,128)(2,1)}, u32[]{:S(2)}) copy-start(bf16[512,3136]{0,1:T(8,128)(2,1)} %param.14) | copy-start | bytes 9633796
Sparse Core Ops, SparseCore 0:
  84.8 183.0 all-reduce.3
where the time goes:
time: 285 us; the launch traced here: 284 us
  waiting for transfers between devices  94.7 us (33%)
  blocking collectives  84.8 us (30%)
  local copies, waits for them, and re-layouts  51.5 us (18%)
  matrix products  23.4 us (8%)
  between operations  16.7 us (6%)
  other arithmetic  12.5 us (4%)
    psum x1, waiting for transfers between devices, on_device(): grad_w1 = lax.psum(local_w1, 'dp')  94.7 us
    pmax x1, blocking collectives, on_device(): top = lax.pmax(local_top, 'dp')  43.8 us
    psum x1, blocking collectives, on_device(): grad_b1, grad_w2, grad_b2 = lax.psum((local_b1, local_w2, local_b2), 'dp')  41 us
    unnamed x27, local copies, waits for them, and re-layouts  16.6 us
    reshape x2, local copies, waits for them, and re-layouts, forward_loss(): (jnp.dot(hidden, w_two, preferred_element_type=jnp.float32) + b_two).resh...  11.3 us
    gather x2, local copies, waits for them, and re-layouts, forward_loss(): jnp.take_along_axis(target_probs, next_action[:, None, None], axis=1)  10.7 us
    gather x1, local copies, waits for them, and re-layouts, forward_loss(): chosen = jnp.take_along_axis(logits, action[:, None, None], axis=1)[:, 0, :]  10.6 us
    dot_general x1, matrix products, on_device(): lax.dot_general(grad_pre, features, (((0,), (0,)), ((), ())), preferred_e...  8.19 us
  transfers between devices with their start and end apart: 1, of which 1 were waited for; matrix products, arithmetic and copies ran while one was open for 1% of the time, Pallas kernels for 0%

commit v1 on v0

--- a/solution.py
+++ b/solution.py
@@ -100,7 +100,15 @@
     local_w1 = lax.dot_general(
         grad_pre, features, (((0,), (0,)), ((), ())), preferred_element_type=jnp.float32
     )
-    grad_w1 = lax.psum(local_w1, "dp")
+    axis_total = lax.axis_size("dp")
+    grad_w1 = local_w1
+    for w in [rr for rr in (1, 2, 4, 8, 16) if rr < axis_total]:
+        frames = []
+        k = 0
+        while k < axis_total:
+            frames.append((k, k ^ w))
+            k = k + 1
+        grad_w1 = grad_w1 + lax.ppermute(grad_w1, axis_name="dp", perm=frames)
     priorities = cross_ent / jnp.maximum(top, 1.0)
     mean_loss = loss_sum / total_rows
     return (grad_w1, grad_b1, grad_w2, grad_b2, mean_loss, priorities)

time: 285 us -> 928 us (3.26)
  waiting for transfers between devices: 94.7 us -> 454 us
  blocking collectives: 84.8 us -> 339 us
  other arithmetic: 12.5 us -> 39.3 us
    ppermute x0 -> x5, waiting for transfers between devices: none -> 425 us  [on_device(): grad_w1 = grad_w1 + lax.ppermute(grad_w1, axis_name='dp', perm=frames)]
    pmax x1, blocking collectives: 43.8 us -> 300 us  [on_device(): top = lax.pmax(local_top, 'dp')]
    psum x1, waiting for transfers between devices: 94.7 us -> 29.5 us  [on_device(): grad_b1, grad_w2, grad_b2 = lax.psum((local_b1, local_w2, local_b2), 'dp')]
    add x0 -> x5, other arithmetic: none -> 26.7 us  [on_device(): grad_w1 = grad_w1 + lax.ppermute(grad_w1, axis_name='dp', perm=frames)]
  transfers between devices with their start and end apart: 1 -> 6, of which waited for: 1 -> 5; matrix products, arithmetic and copies ran while one was open for 1% -> 2% of each run, Pallas kernels for 0% -> 0%
where the time goes in v1:
time: 928 us; the launch traced here: 927 us
  waiting for transfers between devices  454 us (49%)
  blocking collectives  339 us (37%)
  local copies, waits for them, and re-layouts  46.6 us (5%)
  other arithmetic  39.3 us (4%)
  matrix products  22.6 us (2%)
  between operations  16.7 us (2%)
    ppermute x5, waiting for transfers between devices, on_device(): grad_w1 = grad_w1 + lax.ppermute(grad_w1, axis_name='dp', perm=frames)  425 us
    pmax x1, blocking collectives, on_device(): top = lax.pmax(local_top, 'dp')  300 us
    psum x1, blocking collectives, on_device(): grad_b1, grad_w2, grad_b2 = lax.psum((local_b1, local_w2, local_b2), 'dp')  39.2 us
    psum x1, waiting for transfers between devices, on_device(): grad_b1, grad_w2, grad_b2 = lax.psum((local_b1, local_w2, local_b2), 'dp')  29.5 us
    add x5, other arithmetic, on_device(): grad_w1 = grad_w1 + lax.ppermute(grad_w1, axis_name='dp', perm=frames)  26.7 us
  transfers between devices with their start and end apart: 6, of which 5 were waited for; matrix products, arithmetic and copies ran while one was open for 2% of the time, Pallas kernels for 0%

profile of v1, /device:TPU:0, one launch (start us, length us, event | category | flops | bytes accessed | tf_op | source)
XLA Modules:
  0.0 927.4 jit_solution(18053354973743958729)
XLA Ops:
  10.6 5.9 fusion.16
  17.8 3.0 convolution_add_fusion
  20.8 3.9 reshape.118
  24.7 7.5 copy.39
  32.2 10.6 %gather_fusion = f32[1024,51]{1,0:T(8,128)S(1)} fusion(f32[1024,18,51]{2,0,1:T(8,128)} %copy.39, s32[1024]{0:T(1024)S(1)} %bitcast.54), kind=kCustom, calls=%fused_computation.clone | custom fusion | bytes 425984 | tf_op jit(solution)/shard_map/jit(take_along_axis)/gather | solution.py:33
  43.7 7.5 copy.40
  51.2 10.5 %gather_fusion.1 = f32[1024,51]{1,0:T(8,128)S(1)} fusion(f32[1024,18,51]{2,0,1:T(8,128)} %copy.40, s32[1024]{0:T(1024)S(1)} %bitcast.53), kind=kCustom, calls=%fused_computation.1.clone | custom fusion | bytes 425984 | tf_op jit(solution)/shard_map/jit(take_along_axis)/gather | solution.py:35
  62.0 4.5 fusion.1
  70.1 3.8 convert_reduce_fusion.1
  73.9 5.9 fusion.17
  80.4 10.1 %collective-permute-done = f32[512,3136]{0,1:T(8,128)} collective-permute-done((f32[512,3136]{0,1:T(8,128)S(1)}, f32[512,3136]{0,1:T(8,128)}, u32[]{:S(2)}, u32[]{:S(2)}) %collective-permute-start) | collective-permute-done | bytes 6422560 | tf_op jit(solution)/shard_map/ppermute | solution.py:111
  90.5 4.4 add.62
  94.9 2.9 collective-permute-start.1
  97.8 138.7 %collective-permute-done.1 = f32[512,3136]{0,1:T(8,128)} collective-permute-done((f32[512,3136]{0,1:T(8,128)S(1)}, f32[512,3136]{0,1:T(8,128)}, u32[]{:S(2)}, u32[]{:S(2)}) %collective-permute-start.1) | collective-permute-done | bytes 6422560 | tf_op jit(solution)/shard_map/ppermute | solution.py:111
  236.5 4.4 add.63
  242.7 138.2 %collective-permute-done.2 = f32[512,3136]{0,1:T(8,128)} collective-permute-done((f32[512,3136]{0,1:T(8,128)S(1)}, f32[512,3136]{0,1:T(8,128)}, u32[]{:S(2)}, u32[]{:S(2)}) %collective-permute-start.2) | collective-permute-done | bytes 6422560 | tf_op jit(solution)/shard_map/ppermute | solution.py:111
  380.9 4.4 add.64
  386.9 137.5 %collective-permute-done.3 = f32[512,3136]{0,1:T(8,128)S(1)} collective-permute-done((f32[512,3136]{0,1:T(8,128)S(1)}, f32[512,3136]{0,1:T(8,128)S(1)}, u32[]{:S(2)}, u32[]{:S(2)}) %collective-permute-start.3) | collective-permute-done | bytes 6422560 | tf_op jit(solution)/shard_map/ppermute | solution.py:111
  524.3 4.3 add.65
  530.9 4.0 fusion.5
  536.2 299.9 %pmax.7 = f32[]{:T(128)} all-reduce(f32[]{:T(128)} %get-tuple-element.9), channel_id=1, replica_groups=mesh['dp'=32] {'dp'}, use_global_device_ids=true, to_apply=%region_13.15 | all-reduce | flops 1 | bytes 8 | tf_op jit(solution)/shard_map/pmax | solution.py:93
  837.4 39.2 %all-reduce = (f32[512]{0:T(512)}, f32[918]{0:T(1024)}, f32[]{:T(128)}) all-reduce(f32[512]{0:T(512)S(1)} %get-tuple-element.22, f32[918]{0:T(1024)S(1)} %reduce_sum.74, f32[]{:T(128)} %get-tuple-element.10), channel_id=1, replica_groups=mesh['dp'=32] {'dp'}, use_global_device_ids=true, to_apply=%region_5.7 | all-reduce | flops 1431 | bytes 11448 | tf_op jit(solution)/shard_map/psum | solution.py:99
  877.8 9.2 add.66
  887.0 29.5 %all-reduce.3.cloned.1.call-done = f32[512,918]{0,1:T(8,128)} async-done(((f32[512,918]{0,1:T(8,128)}), f32[512,918]{0,1:T(8,128)}) %all-reduce.3.cloned.1.call-update) | async-done | bytes 1880080 | tf_op jit(solution)/shard_map/psum | solution.py:99
  (50 shorter events, 20.9 us)
Async XLA Ops:
  7.2 3.4 copy-start
  7.2 909.3 %all-reduce.3.cloned.1.call-start = ((), (), s32[]{:S(2)}) async-start(), calls=%async_computation | async-start | bytes 3768320 | tf_op jit(solution)/shard_map/psum | solution.py:99
  10.5 7.3 copy-start.6
  10.6 7.3 copy-start.7
  10.6 7.2 copy-start.8
  16.5 1.3 copy-start.9
  51.2 10.8 %copy-start.4 = (f32[1024,51]{0,1:T(8,128)S(1)}, f32[1024,51]{0,1:T(8,128)}, u32[]{:S(2)}) copy-start(f32[1024,51]{0,1:T(8,128)} %param.22) | copy-start | bytes 626692
  51.2 10.8 %copy-start.3 = (s32[1024,51]{0,1:T(8,128)S(1)}, s32[1024,51]{0,1:T(8,128)}, u32[]{:S(2)}) copy-start(s32[1024,51]{0,1:T(8,128)} %param.21) | copy-start | bytes 626692
  51.2 15.5 %copy-start.5 = (f32[1024]{0:T(1024)S(1)}, f32[1024]{0:T(1024)}, u32[]{:S(2)}) copy-start(f32[1024]{0:T(1024)} %param.23) | copy-start | bytes 12292
  79.8 10.6 %collective-permute-start = (f32[512,3136]{0,1:T(8,128)S(1)}, f32[512,3136]{0,1:T(8,128)}, u32[]{:S(2)}, u32[]{:S(2)}) collective-permute-start(f32[512,3136]{0,1:T(8,128)S(1)} %fusion.17), channel_id=1, source_target_pairs={{0,1},{1,0},{2,3},{3,2},{4,5},{5,4},{6,7},{7,6},{8,9},{9,8},{10,11... | collective-permute-start | bytes 19267592 | tf_op jit(solution)/shard_map/ppermute | solution.py:111
  94.9 141.7 %collective-permute-start.1 = (f32[512,3136]{0,1:T(8,128)S(1)}, f32[512,3136]{0,1:T(8,128)}, u32[]{:S(2)}, u32[]{:S(2)}) collective-permute-start(f32[512,3136]{0,1:T(8,128)S(1)} %add.62), channel_id=1, source_target_pairs={{0,2},{1,3},{2,0},{3,1},{4,6},{5,7},{6,4},{7,5},{8,10},{9,11},{10,... | collective-permute-start | bytes 19267592 | tf_op jit(solution)/shard_map/ppermute | solution.py:111
  240.9 140.0 %collective-permute-start.2 = (f32[512,3136]{0,1:T(8,128)S(1)}, f32[512,3136]{0,1:T(8,128)}, u32[]{:S(2)}, u32[]{:S(2)}) collective-permute-start(f32[512,3136]{0,1:T(8,128)S(1)} %add.63), channel_id=1, source_target_pairs={{0,4},{1,5},{2,6},{3,7},{4,0},{5,1},{6,2},{7,3},{8,12},{9,13},{10,... | collective-permute-start | bytes 19267592 | tf_op jit(solution)/shard_map/ppermute | solution.py:111
  385.3 145.6 %copy-start.2 = (bf16[1024,918]{0,1:T(8,128)(2,1)S(1)}, bf16[1024,918]{0,1:T(8,128)(2,1)}, u32[]{:S(2)}) copy-start(bf16[1024,918]{0,1:T(8,128)(2,1)} %convert_element_type.22) | copy-start | bytes 5640196
  385.3 139.0 %collective-permute-start.3 = (f32[512,3136]{0,1:T(8,128)S(1)}, f32[512,3136]{0,1:T(8,128)S(1)}, u32[]{:S(2)}, u32[]{:S(2)}) collective-permute-start(f32[512,3136]{0,1:T(8,128)S(1)} %add.64), channel_id=1, source_target_pairs={{0,8},{1,9},{2,10},{3,11},{4,12},{5,13},{6,14},{7,15},{8,0},{9,1},... | collective-permute-start | bytes 19267592 | tf_op jit(solution)/shard_map/ppermute | solution.py:111
  528.7 349.2 %collective-permute-start.4 = (f32[512,3136]{0,1:T(8,128)}, f32[512,3136]{0,1:T(8,128)}, u32[]{:S(2)}, u32[]{:S(2)}) collective-permute-start(f32[512,3136]{0,1:T(8,128)} %add.65), channel_id=1, source_target_pairs={{0,16},{1,17},{2,18},{3,19},{4,20},{5,21},{6,22},{7,23},{8,24},{9,... | collective-permute-start | bytes 19267592 | tf_op jit(solution)/shard_map/ppermute | solution.py:111
  877.8 41.6 %copy-start.1 = (bf16[512,3136]{0,1:T(8,128)(2,1)S(1)}, bf16[512,3136]{0,1:T(8,128)(2,1)}, u32[]{:S(2)}) copy-start(bf16[512,3136]{0,1:T(8,128)(2,1)} %param.14) | copy-start | bytes 9633796
Sparse Core Ops, SparseCore 0:
  535.1 381.3 all-reduce.2
